TPU v7x, 32 devices: a whole 2x2x4 slice. The times are simulated.
32 devices in a mesh: clip: 2 (over y), outer: 4 (over z), inner: 2 (over x), head: 2 (over core).
Axes of the slice: x: 2, y: 2, z: 4, core: 2. Of those that a mesh axis runs over, the one named last changes fastest.
Arguments:
- tokens: bfloat16 [2, 4096, 3072], P('clip', ('outer', 'inner', 'head')), parts along dimension 0, may hold values from -6 to 6
- shift_mod: float32 [2, 3072], P('clip'), parts along dimension 0, may hold values from -3 to 3
- scale_mod: float32 [2, 3072], P('clip'), parts along dimension 0, may hold values from -1.5 to 1.5
- gate_mod: float32 [2, 3072], P('clip'), parts along dimension 0, may hold values from 0.5 to 2
- query_weight: bfloat16 [3072, 3072], P('outer', ('inner', 'head')), may hold values from -0.109375 to 0.109375
- key_weight: bfloat16 [3072, 3072], P('outer', ('inner', 'head')), may hold values from -0.109375 to 0.109375
- value_weight: bfloat16 [3072, 3072], P('outer', ('inner', 'head')), may hold values from -0.109375 to 0.109375
- out_weight: bfloat16 [3072, 3072], P(('inner', 'head'), 'outer'), may hold values from -0.109375 to 0.109375
- query_gain: float32 [128], replicated, may hold values from 1 to 18, as said below
- key_gain: float32 [128], replicated, may hold values from 1 to 18, as said below
Outputs:
- attended: bfloat16 [2, 4096, 3072], P('clip', ('outer', 'inner', 'head')), parts along dimension 0
There are 2 independent parts, one for each index of `clip`. A program takes and returns all parts, laid end to end along the dimension named above; an argument that names none is the same for every part. Nothing has to cross between parts.
Inputs may be any that keep to these rules, and one draw needn't show every extreme that they name: `query_gain`: 128 positive scales. `key_gain`: 128 positive scales.
All inputs are finite; a program needn't handle non-finite values.
Results may differ from a plain program's by a relative error of at most 0.015.
The roundings to bfloat16 on the way count: a program that leaves them out, or rounds other values in their place, can miss the bound.
Values may be sent and summed in bfloat16 or wider, within the bound.
A program may use at most 192 MiB of HBM per device.

v0:
```python
import math
import jax
import jax.numpy as jnp
from jax import lax
from jax.sharding import PartitionSpec as P

EPSILON = 1e-06


def modulate(tokens, shift_mod, scale_mod):
    values = tokens.astype(jnp.float32)
    center = jnp.mean(values, axis=-1, keepdims=True)
    spread = jnp.mean(jnp.square(values - center), axis=-1, keepdims=True)
    normed = (values - center) / jnp.sqrt(spread + EPSILON)
    return (normed * (1.0 + scale_mod[:, None, :]) + shift_mod[:, None, :]).astype(jnp.bfloat16)


def head_norm(projected, gain_vec, head_dim):
    shaped = projected.reshape(projected.shape[:-1] + (projected.shape[-1] // head_dim, head_dim))
    mean_square = jnp.mean(jnp.square(shaped), axis=-1, keepdims=True)
    return (shaped / jnp.sqrt(mean_square + EPSILON) * gain_vec).astype(jnp.bfloat16)


def per_device(
    tokens,
    shift_mod,
    scale_mod,
    gate_mod,
    query_weight,
    key_weight,
    value_weight,
    out_weight,
    query_gain,
    key_gain,
):
    head_dim = query_gain.shape[0]
    modulated = modulate(tokens, shift_mod, scale_mod)
    gathered = lax.all_gather(modulated, ("inner", "head"), axis=1, tiled=True)
    clip_count, row_count, model_width = gathered.shape
    flattened = gathered.reshape(clip_count * row_count, model_width)
    local_cols = query_weight.shape[1]
    head_count = local_cols // head_dim
    full_query, full_key, full_value = (
        lax.all_gather(query_weight, "outer", axis=0, tiled=True),
        lax.all_gather(key_weight, "outer", axis=0, tiled=True),
        lax.all_gather(value_weight, "outer", axis=0, tiled=True),
    )
    query_proj = jnp.dot(flattened, full_query, preferred_element_type=jnp.float32)
    key_proj = jnp.dot(flattened, full_key, preferred_element_type=jnp.float32)
    value_proj = jnp.dot(flattened, full_value, preferred_element_type=jnp.float32)
    query_heads = head_norm(
        query_proj.reshape(clip_count, row_count, local_cols), query_gain, head_dim
    )
    key_send = head_norm(key_proj.reshape(clip_count, row_count, local_cols), key_gain, head_dim)
    key_send = key_send.reshape(clip_count, row_count, local_cols)
    value_send = value_proj.astype(jnp.bfloat16).reshape(clip_count, row_count, local_cols)
    root_size = math.sqrt(head_dim)
    full_out = lax.all_gather(out_weight, "outer", axis=1, tiled=True)
    running_max = jnp.full((clip_count, head_count, row_count), -1e30, jnp.float32)
    key_piece = lax.all_gather(key_send, "outer", axis=1, tiled=True)
    value_piece = lax.all_gather(value_send, "outer", axis=1, tiled=True)
    key_count = key_piece.shape[1]
    key_piece = key_piece.reshape(clip_count, key_count, head_count, head_dim)
    value_piece = value_piece.reshape(clip_count, key_count, head_count, head_dim)
    scores = (
        jnp.einsum("cqhd,ckhd->chqk", query_heads, key_piece, preferred_element_type=jnp.float32)
        / root_size
    )
    new_max = jnp.maximum(running_max, jnp.max(scores, axis=-1))
    weights = jnp.exp(scores - new_max[..., None])
    new_sum = jnp.sum(weights, axis=-1)
    new_acc = jnp.einsum(
        "chqk,ckhd->chqd",
        weights.astype(jnp.bfloat16),
        value_piece,
        preferred_element_type=jnp.float32,
    )
    head_out = new_acc / new_sum[..., None]
    mixed = (
        jnp.transpose(head_out, (0, 2, 1, 3))
        .reshape(clip_count * row_count, local_cols)
        .astype(jnp.bfloat16)
    )
    partial_value = jnp.dot(mixed, full_out, preferred_element_type=jnp.float32).reshape(
        clip_count, row_count, -1
    )
    summed = lax.psum_scatter(
        partial_value.astype(jnp.bfloat16), ("inner", "head"), scatter_dimension=1, tiled=True
    ).astype(jnp.float32)
    return (summed * gate_mod[:, None, :]).astype(jnp.bfloat16)


def solution(mesh):
    in_specs = (
        P("clip", ("outer", "inner", "head"), None),
        P("clip", None),
        P("clip", None),
        P("clip", None),
        P("outer", ("inner", "head")),
        P("outer", ("inner", "head")),
        P("outer", ("inner", "head")),
        P(("inner", "head"), "outer"),
        P(),
        P(),
    )
    out_specs = P("clip", ("outer", "inner", "head"), None)
    return jax.shard_map(
        per_device, mesh=mesh, in_specs=in_specs, out_specs=out_specs, check_vma=False
    )
```

profile of v0, /device:TPU:0, one launch (start us, length us, event | category | flops | bytes accessed | tf_op | source)
XLA Modules:
  0.0 723.6 jit_solution(17213850684140932397)
XLA Ops:
  7.3 1.7 convert_reduce_fusion
  9.6 1.9 fusion.15
  11.7 0.7 all-gather.16.cloned.1.call-update
  13.0 88.1 %all-gather.14.cloned.1.call-done = bf16[3072,768]{1,0:T(8,128)(2,1)} async-done(((bf16[768,768]{1,0:T(8,128)(2,1)}), bf16[3072,768]{1,0:T(8,128)(2,1)}) %all-gather.14.cloned.1.call-update) | async-done | bytes 4718608 | tf_op jit(solution)/shard_map/all_gather | solution.py:45
  101.1 46.4 %all-gather.10.cloned.1.call-done = bf16[1,1024,3072]{2,1,0:T(8,128)(2,1)} async-done(((bf16[1,256,3072]{2,1,0:T(8,128)(2,1)}), bf16[1,1024,3072]{2,1,0:T(8,128)(2,1)}) %all-gather.10.cloned.1.call-update) | async-done | bytes 6291472 | tf_op jit(solution)/shard_map/all_gather | solution.py:38
  147.4 9.8 %fusion.27 = (f32[1024,768]{0,1:T(8,128)S(1)}, f32[1024,768]{0,1:T(8,128)}) fusion(bf16[3072,768]{1,0:T(8,128)(2,1)} %all-gather.14.cloned.1.call-done, bf16[1,1024,3072]{2,1,0:T(8,128)(2,1)} %all-gather.10.cloned.1.call-done), kind=kOutput, calls=%fused_computation.38 | convolution fusion | flops 4832624640 | bytes 17301504 | tf_op jit(solution)/shard_map/dot_general | solution.py:49
  157.5 3.6 fusion.17
  161.2 77.2 %all-gather.16.cloned.1.call-done = bf16[3072,768]{1,0:T(8,128)(2,1)} async-done(((bf16[768,768]{1,0:T(8,128)(2,1)}), bf16[3072,768]{1,0:T(8,128)(2,1)}) %all-gather.16.cloned.1.call-update) | async-done | bytes 4718608 | tf_op jit(solution)/shard_map/all_gather | solution.py:46
  238.4 9.4 %fusion.20 = bf16[1024,768]{1,0:T(8,128)(2,1)} fusion(bf16[3072,768]{1,0:T(8,128)(2,1)} %all-gather.16.cloned.1.call-done, bf16[1,1024,3072]{2,1,0:T(8,128)(2,1)} %all-gather.10.cloned.1.call-done), kind=kOutput, calls=%fused_computation.26 | convolution fusion | flops 4832624640 | bytes 12582912 | tf_op jit(solution)/shard_map/dot_general | solution.py:50
  247.9 0.7 all-gather.18.cloned.1.call-update
  248.8 78.9 %all-gather.12.cloned.1.call-done = bf16[3072,768]{1,0:T(8,128)(2,1)} async-done(((bf16[768,768]{1,0:T(8,128)(2,1)}), bf16[3072,768]{1,0:T(8,128)(2,1)}) %all-gather.12.cloned.1.call-update) | async-done | bytes 4718608 | tf_op jit(solution)/shard_map/all_gather | solution.py:44
  327.7 10.3 %fusion.28 = (f32[1024,768]{0,1:T(8,128)}, f32[1024,768]{0,1:T(8,128)}) fusion(bf16[3072,768]{1,0:T(8,128)(2,1)} %all-gather.12.cloned.1.call-done, bf16[1,1024,3072]{2,1,0:T(8,128)(2,1)} %all-gather.10.cloned.1.call-done), kind=kOutput, calls=%fused_computation.39 | convolution fusion | flops 4832624640 | bytes 17301504 | tf_op jit(solution)/shard_map/dot_general | solution.py:48
  338.0 2.6 copy.14
  340.6 2.2 reduce_sum.47
  342.9 100.0 %all-gather.20.cloned.1.call-done = bf16[4096,768]{0,1:T(8,128)(2,1)} async-done(((bf16[1024,768]{0,1:T(8,128)(2,1)}), bf16[4096,768]{0,1:T(8,128)(2,1)}) %all-gather.20.cloned.1.call-update) | async-done | bytes 6291472 | tf_op jit(solution)/shard_map/all_gather | solution.py:60
  442.9 39.0 %multiply_reduce_fusion = (f32[6,1024]{1,0:T(8,128)S(1)}, f32[6,1024,4096]{2,1,0:T(8,128)}) fusion(bf16[4096,6,128]{0,2,1:T(8,128)(2,1)} %bitcast.44, f32[1024,6,128]{2,0,1:T(8,128)S(1)} %copy.14, f32[128]{0:T(128)S(1)} %copy-done.3, f32[1024,6]{0,1:T(8,128)S(1)} %add_sqrt_fusion.1), kind=kOutput, calls=%fused_computation.1 | convolution fusion | flops 6495135744 | bytes 110150144 | tf_op jit(solution)/shard_map/cqhd,ckhd->chqk/dot_general | solution.py:66
  481.9 76.0 %all-gather.22.cloned.1.call-done = bf16[4096,768]{1,0:T(8,128)(2,1)} async-done(((bf16[1024,768]{1,0:T(8,128)(2,1)}), bf16[4096,768]{1,0:T(8,128)(2,1)}) %all-gather.22.cloned.1.call-update) | async-done | bytes 6291472 | tf_op jit(solution)/shard_map/all_gather | solution.py:61
  557.9 8.8 %copy.16 = bf16[4096,768]{0,1:T(8,128)(2,1)} copy(bf16[4096,768]{1,0:T(8,128)(2,1)} %all-gather.22.cloned.1.call-done) | data formatting | bytes 12582912 | tf_op jit(solution)/shard_map/all_gather | solution.py:61
  566.6 31.5 %fusion = f32[6,1024]{1,0:T(8,128)S(1)} fusion(f32[6,1024,4096]{2,1,0:T(8,128)} %get-tuple-element.10, f32[6,1024]{1,0:T(8,128)S(1)} %broadcast_maximum_fusion), kind=kLoop, calls=%fused_computation.2 | loop fusion | flops 75491328 | bytes 100712448 | tf_op jit(solution)/shard_map/reduce_sum | solution.py:71
  598.1 35.6 %divide_convert_fusion = bf16[6,1024,128]{1,2,0:T(8,128)(2,1)S(1)} fusion(bf16[4096,6,128]{0,2,1:T(8,128)(2,1)} %bitcast.43, f32[6,1024,4096]{2,1,0:T(8,128)} %get-tuple-element.10, f32[6,1024]{1,0:T(8,128)S(1)} %broadcast_maximum_fusion, f32[6,1024]{1,0:T(8,128)S(1)} %fusion), kind=kOutput, calls=%fused_computation.24 | convolution fusion | flops 6519521280 | bytes 108576768 | tf_op jit(solution)/shard_map/chqk,ckhd->chqd/dot_general | solution.py:72
  633.7 13.3 %all-gather.18.cloned.1.call-done = bf16[768,3072]{1,0:T(8,128)(2,1)} async-done(((bf16[768,768]{1,0:T(8,128)(2,1)}), bf16[768,3072]{1,0:T(8,128)(2,1)}) %all-gather.18.cloned.1.call-update) | async-done | bytes 4718608 | tf_op jit(solution)/shard_map/all_gather | solution.py:58
  647.0 9.4 %convert_bitcast_fusion = bf16[1,1024,3072]{2,1,0:T(8,128)(2,1)} fusion(bf16[1024,768]{0,1:T(8,128)(2,1)S(1)} %bitcast.51, bf16[768,3072]{1,0:T(8,128)(2,1)} %all-gather.18.cloned.1.call-done), kind=kOutput, calls=%fused_computation.11 | convolution fusion | flops 4834983936 | bytes 12582912 | tf_op jit(solution)/shard_map/dot_general | solution.py:84
  656.5 57.4 %reduce-scatter.2.cloned.1.call-done = bf16[1,256,3072]{2,1,0:T(8,128)(2,1)} async-done(((bf16[1,1024,3072]{2,1,0:T(8,128)(2,1)}), bf16[1,256,3072]{2,1,0:T(8,128)(2,1)}) %reduce-scatter.2.cloned.1.call-update) | async-done | bytes 1572880 | tf_op jit(solution)/shard_map/reduce_scatter | solution.py:87
  713.8 2.9 multiply_convert_fusion
  (37 shorter events, 2.7 us)
Async XLA Ops:
  6.5 6.4 copy-start
  6.5 2.5 copy-start.2
  6.5 3.1 copy-start.6
  6.5 3.1 copy-start.4
  6.5 94.5 %all-gather.14.cloned.1.call-start = ((), (), s32[]{:S(2)}) async-start(), calls=%async_computation.3 | async-start | bytes 5898240 | tf_op jit(solution)/shard_map/all_gather | solution.py:45
  7.3 140.1 %all-gather.10.cloned.1.call-start = ((), (), s32[]{:S(2)}) async-start(), calls=%async_computation.1 | async-start | bytes 7864320 | tf_op jit(solution)/shard_map/all_gather | solution.py:38
  11.6 226.8 %all-gather.16.cloned.1.call-start = ((), (), s32[]{:S(2)}) async-start(), calls=%async_computation.4 | async-start | bytes 5898240 | tf_op jit(solution)/shard_map/all_gather | solution.py:46
  12.3 315.3 %all-gather.12.cloned.1.call-start = ((), (), s32[]{:S(2)}) async-start(), calls=%async_computation.2 | async-start | bytes 5898240 | tf_op jit(solution)/shard_map/all_gather | solution.py:44
  12.9 430.0 %all-gather.20.cloned.1.call-start = ((), (), s32[]{:S(2)}) async-start(), calls=%async_computation.7 | async-start | bytes 7864320 | tf_op jit(solution)/shard_map/all_gather | solution.py:60
  161.2 396.7 %all-gather.22.cloned.1.call-start = ((), (), s32[]{:S(2)}) async-start(), calls=%async_computation.8 | async-start | bytes 7864320 | tf_op jit(solution)/shard_map/all_gather | solution.py:61
  247.8 399.2 %all-gather.18.cloned.1.call-start = ((), (), s32[]{:S(2)}) async-start(), calls=%async_computation.5 | async-start | bytes 5898240 | tf_op jit(solution)/shard_map/all_gather | solution.py:58
  248.6 465.3 %reduce-scatter.2.cloned.1.call-start = ((), (), s32[]{:S(2)}) async-start(), calls=%async_computation.6 | async-start | bytes 7864320 | tf_op jit(solution)/shard_map/reduce_scatter | solution.py:87
  340.6 102.2 %copy-start.3 = (f32[128]{0:T(128)S(1)}, f32[128]{0:T(128)}, u32[]{:S(2)}) copy-start(f32[128]{0:T(128)} %param.18) | copy-start | bytes 1540
  656.4 57.4 %copy-start.5 = (f32[1,3072]{1,0:T(1,128)S(1)}, f32[1,3072]{1,0:T(1,128)}, u32[]{:S(2)}) copy-start(f32[1,3072]{1,0:T(1,128)} %param.13) | copy-start | bytes 36868
  656.4 60.3 %copy-start.1 = (f32[128]{0:T(128)S(1)}, f32[128]{0:T(128)}, u32[]{:S(2)}) copy-start(f32[128]{0:T(128)} %param.19) | copy-start | bytes 1540
Sparse Core Ops, SparseCore 0:
  8.9 92.0 all-gather.13
  102.6 44.7 all-gather.9
  149.0 89.3 all-gather.15
  239.8 87.7 all-gather.11
  329.1 113.7 all-gather.19
  444.3 113.5 all-gather.21
  559.4 87.5 all-gather.17
  656.6 57.2 reduce-scatter.1
where the time goes:
time: 724 us
  waiting for transfers between devices  540 us (75%)
  matrix products  113 us (16%)
  other arithmetic  44.7 us (6%)
  between operations  13.6 us (2%)
  local copies, waits for them, and re-layouts  11.4 us (2%)
    all_gather x1, waiting for transfers between devices, per_device(): key_piece = lax.all_gather(key_send, 'outer', axis=1, tiled=True)  100 us
    all_gather x1, waiting for transfers between devices, per_device(): lax.all_gather(key_weight, 'outer', axis=0, tiled=True)  88.1 us
    all_gather x1, waiting for transfers between devices, per_device(): lax.all_gather(query_weight, 'outer', axis=0, tiled=True)  78.9 us
    all_gather x1, waiting for transfers between devices, per_device(): lax.all_gather(value_weight, 'outer', axis=0, tiled=True)  77.2 us
    all_gather x1, waiting for transfers between devices, per_device(): value_piece = lax.all_gather(value_send, 'outer', axis=1, tiled=True)  76 us
    reduce_scatter x1, waiting for transfers between devices, per_device(): lax.psum_scatter(partial_value.astype(jnp.bfloat16), ('inner', 'head'), s...  57.4 us
    all_gather x1, waiting for transfers between devices, per_device(): gathered = lax.all_gather(modulated, ('inner', 'head'), axis=1, tiled=True)  46.4 us
    dot_general x1, matrix products, per_device(): jnp.einsum('cqhd,ckhd->chqk', query_heads, key_piece, preferred_element_t...  39 us
  transfers between devices with their start and end apart: 8, of which 8 were waited for; matrix products, arithmetic and copies ran while one was open for 22% of the time, Pallas kernels for 0%

commit v1 on v0

--- a/solution.py
+++ b/solution.py
@@ -5,6 +5,17 @@
 from jax.sharding import PartitionSpec as P
 
 EPSILON = 1e-06
+
+
+def around_the_ring(block, axis, dim):
+    size = lax.axis_size(axis)
+    right = [(i, (i + 1) % size) for i in range(size)]
+    blocks = [block]
+    for reach in range(1, size):
+        blocks = [lax.ppermute(blocks[0], axis, right), *blocks]
+    whole = jnp.concatenate(blocks, axis=dim)
+    shift = (lax.axis_index(axis) + 1) * blocks[-1].shape[dim]
+    return jnp.roll(whole, shift, axis=dim)
 
 
 def modulate(tokens, shift_mod, scale_mod):
@@ -58,7 +69,7 @@
     full_out = lax.all_gather(out_weight, "outer", axis=1, tiled=True)
     running_max = jnp.full((clip_count, head_count, row_count), -1e30, jnp.float32)
     key_piece = lax.all_gather(key_send, "outer", axis=1, tiled=True)
-    value_piece = lax.all_gather(value_send, "outer", axis=1, tiled=True)
+    value_piece = around_the_ring(value_send, "outer", 1)
     key_count = key_piece.shape[1]
     key_piece = key_piece.reshape(clip_count, key_count, head_count, head_dim)
     value_piece = value_piece.reshape(clip_count, key_count, head_count, head_dim)

time: 724 us -> 725 us (level)
  waiting for transfers between devices: 540 us -> 491 us
  starting transfers between devices: 0.49 us -> 39 us
  local copies, waits for them, and re-layouts: 11.4 us -> 22 us
    ppermute x0 -> x3, waiting for transfers between devices: none -> 181 us  [around_the_ring(): blocks = [lax.ppermute(blocks[0], axis, right), *blocks]]
    all_gather x1, waiting for transfers between devices: 78.9 us -> 0.01 us  [per_device(): lax.all_gather(query_weight, 'outer', axis=0, tiled=True)]
    all_gather x1 -> x0, waiting for transfers between devices: 76 us -> none  [per_device(): value_piece = lax.all_gather(value_send, 'outer', axis=1, tiled=True)]
    all_gather x1, waiting for transfers between devices: 100 us -> 28.3 us  [per_device(): key_piece = lax.all_gather(key_send, 'outer', axis=1, tiled=True)]
    ppermute x0 -> x3, starting transfers between devices: none -> 38.7 us  [around_the_ring(): blocks = [lax.ppermute(blocks[0], axis, right), *blocks]]
    all_gather x1, waiting for transfers between devices: 13.3 us -> 0.02 us  [per_device(): full_out = lax.all_gather(out_weight, 'outer', axis=1, tiled=True)]
    reduce_scatter x1, waiting for transfers between devices: 57.4 us -> 70 us  [per_device(): lax.psum_scatter(partial_value.astype(jnp.bfloat16), ('inner', 'head'), s...]
    dynamic_slice x0 -> x2, local copies, waits for them, and re-layouts: none -> 11.9 us  [around_the_ring(): return jnp.roll(whole, shift, axis=dim)]
  transfers between devices with their start and end apart: 8 -> 10, of which waited for: 8 -> 8; matrix products, arithmetic and copies ran while one was open for 22% -> 23% of each run, Pallas kernels for 0% -> 0%
where the time goes in v1:
time: 725 us
  waiting for transfers between devices  491 us (68%)
  matrix products  112 us (15%)
  other arithmetic  47.3 us (7%)
  starting transfers between devices  39 us (5%)
  local copies, waits for them, and re-layouts  22 us (3%)
  between operations  13.7 us (2%)
    ppermute x3, waiting for transfers between devices, around_the_ring(): blocks = [lax.ppermute(blocks[0], axis, right), *blocks]  181 us
    all_gather x1, waiting for transfers between devices, per_device(): lax.all_gather(key_weight, 'outer', axis=0, tiled=True)  85.3 us
    all_gather x1, waiting for transfers between devices, per_device(): lax.all_gather(value_weight, 'outer', axis=0, tiled=True)  77.2 us
    reduce_scatter x1, waiting for transfers between devices, per_device(): lax.psum_scatter(partial_value.astype(jnp.bfloat16), ('inner', 'head'), s...  70 us
    all_gather x1, waiting for transfers between devices, per_device(): gathered = lax.all_gather(modulated, ('inner', 'head'), axis=1, tiled=True)  46.4 us
    ppermute x3, starting transfers between devices, around_the_ring(): blocks = [lax.ppermute(blocks[0], axis, right), *blocks]  38.7 us
    dot_general x1, matrix products, per_device(): jnp.einsum('cqhd,ckhd->chqk', query_heads, key_piece, preferred_element_t...  38.6 us
    dot_general x1, matrix products, per_device(): jnp.einsum('chqk,ckhd->chqd', weights.astype(jnp.bfloat16), value_piece,...  35.5 us
  transfers between devices with their start and end apart: 10, of which 8 were waited for; matrix products, arithmetic and copies ran while one was open for 23% of the time, Pallas kernels for 0%

profile of v1, /device:TPU:0, one launch (start us, length us, event | category | flops | bytes accessed | tf_op | source)
XLA Modules:
  0.0 724.7 jit_solution(4443547460985664975)
XLA Ops:
  11.7 2.6 fusion.15
  15.8 85.3 %all-gather.12.cloned.1.call-done = bf16[3072,768]{1,0:T(8,128)(2,1)} async-done(((bf16[768,768]{1,0:T(8,128)(2,1)}), bf16[3072,768]{1,0:T(8,128)(2,1)}) %all-gather.12.cloned.1.call-update) | async-done | bytes 4718608 | tf_op jit(solution)/shard_map/all_gather | solution.py:56
  101.0 46.4 %all-gather.8.cloned.1.call-done = bf16[1,1024,3072]{2,1,0:T(8,128)(2,1)} async-done(((bf16[1,256,3072]{2,1,0:T(8,128)(2,1)}), bf16[1,1024,3072]{2,1,0:T(8,128)(2,1)}) %all-gather.8.cloned.1.call-update) | async-done | bytes 6291472 | tf_op jit(solution)/shard_map/all_gather | solution.py:49
  147.4 9.8 %fusion.30 = (f32[1024,768]{0,1:T(8,128)S(1)}, f32[1024,768]{0,1:T(8,128)}) fusion(bf16[3072,768]{1,0:T(8,128)(2,1)} %all-gather.12.cloned.1.call-done, bf16[1,1024,3072]{2,1,0:T(8,128)(2,1)} %all-gather.8.cloned.1.call-done), kind=kOutput, calls=%fused_computation.48 | convolution fusion | flops 4832624640 | bytes 17301504 | tf_op jit(solution)/shard_map/dot_general | solution.py:60
  157.5 3.6 fusion.17
  161.2 77.2 %all-gather.14.cloned.1.call-done = bf16[3072,768]{1,0:T(8,128)(2,1)} async-done(((bf16[768,768]{1,0:T(8,128)(2,1)}), bf16[3072,768]{1,0:T(8,128)(2,1)}) %all-gather.14.cloned.1.call-update) | async-done | bytes 4718608 | tf_op jit(solution)/shard_map/all_gather | solution.py:57
  238.4 8.5 %fusion.26 = bf16[1,1024,768]{2,1,0:T(8,128)(2,1)S(1)} fusion(bf16[3072,768]{1,0:T(8,128)(2,1)} %all-gather.14.cloned.1.call-done, bf16[1,1024,3072]{2,1,0:T(8,128)(2,1)} %all-gather.8.cloned.1.call-done), kind=kOutput, calls=%fused_computation.30 | convolution fusion | flops 4832624640 | bytes 12582912 | tf_op jit(solution)/shard_map/dot_general | solution.py:61
  248.1 72.3 %collective-permute-done = bf16[1,1024,768]{2,1,0:T(8,128)(2,1)S(1)} collective-permute-done((bf16[1,1024,768]{2,1,0:T(8,128)(2,1)S(1)}, bf16[1,1024,768]{2,1,0:T(8,128)(2,1)S(1)}, u32[]{:S(2)}, u32[]{:S(2)}) %collective-permute-start) | collective-permute-done | bytes 1572896 | tf_op jit(solution)/shard_map/ppermute | solution.py:15
  320.4 30.5 %collective-permute-start.1 = (bf16[1,1024,768]{2,1,0:T(8,128)(2,1)S(1)}, bf16[1,1024,768]{2,1,0:T(8,128)(2,1)}, u32[]{:S(2)}, u32[]{:S(2)}) collective-permute-start(bf16[1,1024,768]{2,1,0:T(8,128)(2,1)S(1)} %collective-permute-done), channel_id=1, source_target_pairs={{0,4},{4,8},{8,12},{12,0},{1,5},{5,9},{9,13},{13,1},{2,6},{6,10},{... | collective-permute-start | bytes 4718600 | tf_op jit(solution)/shard_map/ppermute | solution.py:15
  351.0 55.7 %collective-permute-done.1 = bf16[1,1024,768]{2,1,0:T(8,128)(2,1)} collective-permute-done((bf16[1,1024,768]{2,1,0:T(8,128)(2,1)S(1)}, bf16[1,1024,768]{2,1,0:T(8,128)(2,1)}, u32[]{:S(2)}, u32[]{:S(2)}) %collective-permute-start.1) | collective-permute-done | bytes 1572896 | tf_op jit(solution)/shard_map/ppermute | solution.py:15
  406.7 8.3 %collective-permute-start.2 = (bf16[1,1024,768]{2,1,0:T(8,128)(2,1)}, bf16[1,1024,768]{2,1,0:T(8,128)(2,1)}, u32[]{:S(2)}, u32[]{:S(2)}) collective-permute-start(bf16[1,1024,768]{2,1,0:T(8,128)(2,1)} %collective-permute-done.1), channel_id=1, source_target_pairs={{0,4},{4,8},{8,12},{12,0},{1,5},{5,9},{9,13},{13,1},{2,6},{6,10},{... | collective-permute-start | bytes 4718600 | tf_op jit(solution)/shard_map/ppermute | solution.py:15
  414.9 10.3 %fusion.31 = (f32[1024,768]{0,1:T(8,128)}, f32[1024,768]{0,1:T(8,128)}) fusion(bf16[3072,768]{1,0:T(8,128)(2,1)} %all-gather.10.cloned.1.call-done, bf16[1,1024,3072]{2,1,0:T(8,128)(2,1)} %all-gather.8.cloned.1.call-done), kind=kOutput, calls=%fused_computation.49 | convolution fusion | flops 4832624640 | bytes 17301504 | tf_op jit(solution)/shard_map/dot_general | solution.py:59
  425.2 2.4 copy.13
  427.6 2.2 reduce_sum.47
  429.9 53.5 %collective-permute-done.2 = bf16[1,1024,768]{2,1,0:T(8,128)(2,1)} collective-permute-done((bf16[1,1024,768]{2,1,0:T(8,128)(2,1)}, bf16[1,1024,768]{2,1,0:T(8,128)(2,1)}, u32[]{:S(2)}, u32[]{:S(2)}) %collective-permute-start.2) | collective-permute-done | bytes 1572896 | tf_op jit(solution)/shard_map/ppermute | solution.py:15
  489.9 3.1 constant_dynamic-slice_fusion
  493.0 8.8 %copy.15 = bf16[1,4096,768]{1,2,0:T(8,128)(2,1)} copy(bf16[1,4096,768]{2,1,0:T(8,128)(2,1)} %constant_dynamic-slice_fusion) | data formatting | bytes 12582912 | tf_op jit(solution)/shard_map/jit(_roll_dynamic)/dynamic_slice | solution.py:18
  501.8 28.3 %all-gather.18.cloned.1.call-done = bf16[4096,768]{0,1:T(8,128)(2,1)} async-done(((bf16[1024,768]{0,1:T(8,128)(2,1)}), bf16[4096,768]{0,1:T(8,128)(2,1)}) %all-gather.18.cloned.1.call-update) | async-done | bytes 6291472 | tf_op jit(solution)/shard_map/all_gather | solution.py:71
  530.1 38.6 %multiply_reduce_fusion = (f32[6,1024]{1,0:T(8,128)S(1)}, f32[6,1024,4096]{2,1,0:T(8,128)}) fusion(bf16[4096,6,128]{0,2,1:T(8,128)(2,1)} %bitcast.48, f32[1024,6,128]{2,0,1:T(8,128)S(1)} %copy.13, f32[128]{0:T(128)S(1)} %copy-done.7, f32[1024,6]{0,1:T(8,128)S(1)} %add_sqrt_fusion.1), kind=kOutput, calls=%fused_computation.1 | convolution fusion | flops 6495135744 | bytes 110150144 | tf_op jit(solution)/shard_map/cqhd,ckhd->chqk/dot_general | solution.py:77
  568.8 31.2 %fusion = f32[6,1024]{1,0:T(8,128)S(1)} fusion(f32[6,1024,4096]{2,1,0:T(8,128)} %get-tuple-element.10, f32[6,1024]{1,0:T(8,128)S(1)} %broadcast_maximum_fusion), kind=kLoop, calls=%fused_computation.2 | loop fusion | flops 75491328 | bytes 100712448 | tf_op jit(solution)/shard_map/reduce_sum | solution.py:82
  600.0 35.5 %divide_convert_fusion = bf16[6,1024,128]{1,2,0:T(8,128)(2,1)S(1)} fusion(bf16[4096,6,128]{0,2,1:T(8,128)(2,1)} %bitcast.47, f32[6,1024,4096]{2,1,0:T(8,128)} %get-tuple-element.10, f32[6,1024]{1,0:T(8,128)S(1)} %broadcast_maximum_fusion, f32[6,1024]{1,0:T(8,128)S(1)} %fusion), kind=kOutput, calls=%fused_computation.24 | convolution fusion | flops 6519521280 | bytes 108576768 | tf_op jit(solution)/shard_map/chqk,ckhd->chqd/dot_general | solution.py:83
  635.6 9.4 %convert_bitcast_fusion = bf16[1,1024,3072]{2,1,0:T(8,128)(2,1)} fusion(bf16[1024,768]{0,1:T(8,128)(2,1)S(1)} %bitcast.55, bf16[768,3072]{1,0:T(8,128)(2,1)} %all-gather.16.cloned.1.call-done), kind=kOutput, calls=%fused_computation.11 | convolution fusion | flops 4834983936 | bytes 12582912 | tf_op jit(solution)/shard_map/dot_general | solution.py:95
  645.0 70.0 %reduce-scatter.2.cloned.1.call-done = bf16[1,256,3072]{2,1,0:T(8,128)(2,1)} async-done(((bf16[1,1024,3072]{2,1,0:T(8,128)(2,1)}), bf16[1,256,3072]{2,1,0:T(8,128)(2,1)}) %reduce-scatter.2.cloned.1.call-update) | async-done | bytes 1572880 | tf_op jit(solution)/shard_map/reduce_scatter | solution.py:98
  715.0 2.9 multiply_convert_fusion
  (53 shorter events, 14.7 us)
Async XLA Ops:
  6.5 9.2 %copy-start = (f32[128]{0:T(128)S(1)}, f32[128]{0:T(128)}, u32[]{:S(2)}) copy-start(f32[128]{0:T(128)} %param.19) | copy-start | bytes 1540
  6.5 5.2 copy-start.2
  6.5 94.5 %all-gather.12.cloned.1.call-start = ((), (), s32[]{:S(2)}) async-start(), calls=%async_computation.3 | async-start | bytes 5898240 | tf_op jit(solution)/shard_map/all_gather | solution.py:56
  7.3 140.1 %all-gather.8.cloned.1.call-start = ((), (), s32[]{:S(2)}) async-start(), calls=%async_computation.1 | async-start | bytes 7864320 | tf_op jit(solution)/shard_map/all_gather | solution.py:49
  14.4 224.0 %all-gather.14.cloned.1.call-start = ((), (), s32[]{:S(2)}) async-start(), calls=%async_computation.4 | async-start | bytes 5898240 | tf_op jit(solution)/shard_map/all_gather | solution.py:57
  15.1 399.8 %all-gather.10.cloned.1.call-start = ((), (), s32[]{:S(2)}) async-start(), calls=%async_computation.2 | async-start | bytes 5898240 | tf_op jit(solution)/shard_map/all_gather | solution.py:55
  15.7 514.4 %all-gather.18.cloned.1.call-start = ((), (), s32[]{:S(2)}) async-start(), calls=%async_computation.7 | async-start | bytes 7864320 | tf_op jit(solution)/shard_map/all_gather | solution.py:71
  161.1 474.4 %all-gather.16.cloned.1.call-start = ((), (), s32[]{:S(2)}) async-start(), calls=%async_computation.5 | async-start | bytes 5898240 | tf_op jit(solution)/shard_map/all_gather | solution.py:69
  246.9 1.1 copy-start.3
  248.1 72.3 %collective-permute-start = (bf16[1,1024,768]{2,1,0:T(8,128)(2,1)S(1)}, bf16[1,1024,768]{2,1,0:T(8,128)(2,1)S(1)}, u32[]{:S(2)}, u32[]{:S(2)}) collective-permute-start(bf16[1,1024,768]{2,1,0:T(8,128)(2,1)S(1)} %fusion.26), channel_id=1, source_target_pairs={{0,4},{4,8},{8,12},{12,0},{1,5},{5,9},{9,13},{13,1},{2,6},{6,10},{... | collective-permute-start | bytes 4718600 | tf_op jit(solution)/shard_map/ppermute | solution.py:15
  320.4 104.8 %copy-start.5 = (bf16[1,1024,768]{2,1,0:T(8,128)(2,1)}, bf16[1,1024,768]{2,1,0:T(8,128)(2,1)S(1)}, u32[]{:S(2)}) copy-start(bf16[1,1024,768]{2,1,0:T(8,128)(2,1)S(1)} %collective-permute-done) | copy-start | bytes 4718596
  320.4 86.2 %collective-permute-start.1 = (bf16[1,1024,768]{2,1,0:T(8,128)(2,1)S(1)}, bf16[1,1024,768]{2,1,0:T(8,128)(2,1)}, u32[]{:S(2)}, u32[]{:S(2)}) collective-permute-start(bf16[1,1024,768]{2,1,0:T(8,128)(2,1)S(1)} %collective-permute-done), channel_id=1, source_target_pairs={{0,4},{4,8},{8,12},{12,0},{1,5},{5,9},{9,13},{13,1},{2,6},{6,10},{... | collective-permute-start | bytes 4718600 | tf_op jit(solution)/shard_map/ppermute | solution.py:15
  350.9 364.1 %reduce-scatter.2.cloned.1.call-start = ((), (), s32[]{:S(2)}) async-start(), calls=%async_computation.6 | async-start | bytes 7864320 | tf_op jit(solution)/shard_map/reduce_scatter | solution.py:98
  406.7 76.7 %collective-permute-start.2 = (bf16[1,1024,768]{2,1,0:T(8,128)(2,1)}, bf16[1,1024,768]{2,1,0:T(8,128)(2,1)}, u32[]{:S(2)}, u32[]{:S(2)}) collective-permute-start(bf16[1,1024,768]{2,1,0:T(8,128)(2,1)} %collective-permute-done.1), channel_id=1, source_target_pairs={{0,4},{4,8},{8,12},{12,0},{1,5},{5,9},{9,13},{13,1},{2,6},{6,10},{... | collective-permute-start | bytes 4718600 | tf_op jit(solution)/shard_map/ppermute | solution.py:15
  429.8 56.6 %copy-start.6 = (bf16[1,1024,768]{2,1,0:T(8,128)(2,1)S(1)}, bf16[1,1024,768]{2,1,0:T(8,128)(2,1)}, u32[]{:S(2)}) copy-start(bf16[1,1024,768]{2,1,0:T(8,128)(2,1)} %copy-done.5) | copy-start | bytes 4718596
  429.9 56.7 %copy-start.4 = (bf16[1,1024,768]{2,1,0:T(8,128)(2,1)S(1)}, bf16[1,1024,768]{2,1,0:T(8,128)(2,1)}, u32[]{:S(2)}) copy-start(bf16[1,1024,768]{2,1,0:T(8,128)(2,1)} %copy-done.3) | copy-start | bytes 4718596
  493.0 37.1 %copy-start.7 = (f32[128]{0:T(128)S(1)}, f32[128]{0:T(128)}, u32[]{:S(2)}) copy-start(f32[128]{0:T(128)} %param.18) | copy-start | bytes 1540
  645.0 70.0 %copy-start.8 = (f32[1,3072]{1,0:T(1,128)S(1)}, f32[1,3072]{1,0:T(1,128)}, u32[]{:S(2)}) copy-start(f32[1,3072]{1,0:T(1,128)} %param.13) | copy-start | bytes 36868
  645.0 72.9 %copy-start.1 = (f32[128]{0:T(128)S(1)}, f32[128]{0:T(128)}, u32[]{:S(2)}) copy-start(f32[128]{0:T(128)} %param.19) | copy-start | bytes 1540
Sparse Core Ops, SparseCore 0:
  8.9 92.1 all-gather.11
  102.6 44.7 all-gather.7
  149.0 89.3 all-gather.13
  239.8 130.4 all-gather.9
  371.8 158.2 all-gather.17
  531.5 87.5 all-gather.15
  645.1 69.8 reduce-scatter.1
